TPU v7x, 32 devices: a whole 2x2x4 slice. The times are simulated.
32 devices in a mesh: chain: 8 (over y, x, core), par: 4 (over z).
Axes of the slice: x: 2, y: 2, z: 4, core: 2. Of those that a mesh axis runs over, the one named last changes fastest.
Arguments:
- propagation_gains: bfloat16 [4, 16, 64, 8192], P('par', None, None, 'chain'), may hold values from -0.13258252 to 0.13258252, as said below
- observed_samples: bfloat16 [4, 16, 32, 8192], P('par', None, None, 'chain'), may hold values from -6 to 6
- disturbance_variance: float32 [4, 16], P(None, 'chain'), may hold values from 0.05 to 0.5
- retained_branches: int32 [4, 16, 16, 1024], P(None, 'chain', 'par'), may hold values from 0 to 63
Outputs:
- distances: float32 [4, 16, 16, 1024], P(None, 'chain', 'par')
Inputs may be any that keep to these rules, and one draw needn't show every extreme that they name: `propagation_gains`: row 2u holds the real and row 2u+1 the imaginary part of the channel to user u.
All inputs are finite; a program needn't handle non-finite values.
Results may differ from a plain program's by a relative error of at most 0.0003.
Values sent between devices are 32-bit elements; how exact they have to be, the bound alone decides.
A program may use at most 64 MiB of HBM per device.

v0:
```python
import jax
import jax.numpy as jnp
from jax import lax
from jax.sharding import PartitionSpec as P

constellation_norm = 1.0 / 42.0**0.5


def prefix(x, axis, combine, identity):
    length, here = (lax.axis_size(axis), lax.axis_index(axis))
    everything = jax.tree.map(lambda part: lax.all_gather(part, axis), x)
    start = jax.tree.map(
        lambda part, zero: jnp.broadcast_to(jnp.asarray(zero, part.dtype), part.shape), x, identity
    )

    def turn(k, before):
        reached = k < here
        new = combine(before, jax.tree.map(lambda part: part[k], everything))
        return jax.tree.map(lambda a, b: jnp.where(reached, a, b), new, before)

    return lax.fori_loop(0, length, turn, start)


def from_root(block, axis, owner):
    block = jnp.where(lax.axis_index(axis) == owner, block, jnp.zeros_like(block))
    return lax.psum(block, axis)


def fold_stats(raw_gram, raw_cross):
    outer_dimensions = raw_gram.shape[:-2]
    terminal_number = raw_gram.shape[-1] // 2
    pieces = raw_gram.reshape(outer_dimensions + (terminal_number, 2, terminal_number, 2))
    same_part = pieces[..., :, 0, :, 0] + pieces[..., :, 1, :, 1]
    cross_part = pieces[..., :, 1, :, 0] - pieces[..., :, 0, :, 1]
    crossed = raw_cross.reshape(outer_dimensions + (terminal_number, 2, -1, 2))
    rhs_real = crossed[..., :, 0, :, 0] + crossed[..., :, 1, :, 1]
    rhs_imag = crossed[..., :, 0, :, 1] - crossed[..., :, 1, :, 0]
    rhs = jnp.stack([rhs_real, rhs_imag], axis=-2).reshape(
        outer_dimensions + (2 * terminal_number, -1)
    )
    return (same_part, cross_part, rhs)


def assemble(same_part, cross_part, noise):
    row_even = jnp.stack([same_part, cross_part], axis=-1)
    row_odd = jnp.stack([-cross_part, same_part], axis=-1)
    whole = jnp.stack([row_even, row_odd], axis=-3)
    order = 2 * same_part.shape[-1]
    gram = whole.reshape(same_part.shape[:-2] + (order, order))
    return gram + noise[..., None, None] * jnp.eye(order, dtype=jnp.float32)


def estimate_transmitted(cholesky_triangle, whitened_observation, retained_branches):
    terminal_number = cholesky_triangle.shape[-1] // 2
    outer_dimensions = retained_branches.shape[:-1]
    kept_branch_number = retained_branches.shape[-1] // terminal_number
    constellation_position = retained_branches.reshape(
        outer_dimensions + (kept_branch_number, terminal_number)
    )
    inphase_amplitude = (2 * (constellation_position % 8) - 7).astype(jnp.float32)
    quadrature_amplitude = (2 * (constellation_position // 8) - 7).astype(jnp.float32)
    branch_vector = (
        jnp.stack([inphase_amplitude, quadrature_amplitude], axis=-1).reshape(
            outer_dimensions + (kept_branch_number, 2 * terminal_number)
        )
        * constellation_norm
    )
    upper_factor = jnp.swapaxes(cholesky_triangle, -1, -2)
    mapped = jnp.einsum(
        "bsij,bstkj->bstki", upper_factor, branch_vector, precision=lax.Precision.HIGHEST
    )
    remainder_error = jnp.swapaxes(whitened_observation, -1, -2)[..., None, :] - mapped
    squared_errors = (
        (remainder_error * remainder_error)
        .reshape(outer_dimensions + (kept_branch_number, terminal_number, 2))
        .sum(axis=-1)
    )
    accrued_metric = jnp.cumsum(squared_errors[..., ::-1], axis=-1)[..., ::-1] / terminal_number
    return accrued_metric.reshape(outer_dimensions + (kept_branch_number * terminal_number,))


def add_tree(earlier, later):
    return jax.tree.map(jnp.add, earlier, later)


def flatten_last(array_in):
    return array_in.reshape(array_in.shape[:2] + (-1,))


def local(propagation_gains, observed_samples, disturbance_variance, retained_branches):
    terminal_number = propagation_gains.shape[2] // 2
    sym_total = observed_samples.shape[2] // 2
    clusters = lax.axis_size("chain")
    sub_share = propagation_gains.shape[1] // clusters
    raw_gram = jnp.einsum(
        "bsra,bsqa->bsrq", propagation_gains, propagation_gains, preferred_element_type=jnp.float32
    )
    raw_cross = jnp.einsum(
        "bsra,bsqa->bsrq", propagation_gains, observed_samples, preferred_element_type=jnp.float32
    )
    statistic = (flatten_last(raw_gram), flatten_last(raw_cross))
    zeros_tree = jax.tree.map(jnp.zeros_like, statistic)
    earlier = prefix(statistic, "chain", add_tree, zeros_tree)
    running = add_tree(earlier, statistic)
    totals = jax.tree.map(lambda part: from_root(part, "chain", clusters - 1), running)
    start = lax.axis_index("chain") * sub_share
    shares = jax.tree.map(
        lambda whole: lax.dynamic_slice_in_dim(whole, start, sub_share, 1), totals
    )
    outer_dimensions = (1, sub_share)
    same_part, cross_part, rhs = fold_stats(
        shares[0].reshape(outer_dimensions + (2 * terminal_number, 2 * terminal_number)),
        shares[1].reshape(outer_dimensions + (2 * terminal_number, 2 * sym_total)),
    )
    band_index = lax.axis_index("par")
    own_noise = lax.dynamic_slice_in_dim(disturbance_variance, band_index, 1, 0)
    lower_own = jnp.linalg.cholesky(assemble(same_part, cross_part, own_noise))
    rotated_own = jax.scipy.linalg.solve_triangular(lower_own, rhs, lower=True)
    cholesky_triangle = lax.all_gather(lower_own, "par", axis=0, tiled=True)
    whitened_observation = lax.all_to_all(
        rotated_own, "par", split_axis=3, concat_axis=0, tiled=True
    )
    return estimate_transmitted(cholesky_triangle, whitened_observation, retained_branches)


def solution(mesh):
    placed = (
        P("par", None, None, "chain"),
        P("par", None, None, "chain"),
        P(None, "chain"),
        P(None, "chain", "par", None),
    )
    return jax.shard_map(
        local, mesh=mesh, in_specs=placed, out_specs=P(None, "chain", "par", None), check_vma=False
    )
```

profile of v0, /device:TPU:0, one launch (start us, length us, event | category | flops | bytes accessed | tf_op | source)
XLA Modules:
  0.0 226.0 jit_solution(8765339987140583563)
XLA Ops:
  6.5 1.6 copy-done
  8.1 1.9 fusion
  10.0 0.9 all_gather_reshape.7
  11.0 0.7 fusion.2
  11.7 0.9 all_gather_reshape.6
  12.7 0.9 reshape.316
  13.6 0.9 reshape.314
  14.5 0.7 copy.125
  15.1 1.1 reshape.317
  16.2 0.5 fusion.10
  16.8 0.2 maximum_multiply_fusion
  17.0 1.3 copy.136
  18.3 0.2 dynamic-slice_reduce_fusion
  18.5 18.7 %all-gather.5.cloned.1.call-done = f32[8,1,16,2048]{3,2,1,0:T(8,128)} async-done(((f32[1,1,16,2048]{3,2,1,0:T(8,128)}), f32[8,1,16,2048]{3,2,1,0:T(8,128)}) %all-gather.5.cloned.1.call-update) | async-done | bytes 1048592 | tf_op jit(solution)/shard_map/all_gather | solution.py:11
  37.2 29.7 %all-gather.3.cloned.1.call-done = f32[8,1,16,4096]{3,2,1,0:T(8,128)} async-done(((f32[1,1,16,4096]{3,2,1,0:T(8,128)}), f32[8,1,16,4096]{3,2,1,0:T(8,128)}) %all-gather.3.cloned.1.call-update) | async-done | bytes 2097168 | tf_op jit(solution)/shard_map/all_gather | solution.py:11
  66.9 16.1 %while.16 = (s32[]{:T(128)}, f32[1,16,4096]{2,1,0:T(8,128)S(1)}, f32[1,16,2048]{2,1,0:T(8,128)S(1)}, s32[]{:T(128)}, f32[8,1,16,4096]{3,2,1,0:T(8,128)}, /*index=5*/f32[8,1,16,2048]{3,2,1,0:T(8,128)}, s32[]{:T(128)}, s32[]{:T(128)}) while((s32[]{:T(128)}, f32[1,16,4096]{2,1,0:T(8,128)S(1)}, f32[1,16,2048]{2,1,0:T(8,128)S(1)}, ...), condition=%wide.region_1.2_spmd.clone, body=%wide.region_0.1_spmd.clone.sunk | while | flops 294916 | bytes 1179771 | solution.py:21
  66.9 1.0 add_select_fusion.9
  67.9 1.0 add_select_fusion.8
  69.0 0.9 add_select_fusion.9
  69.9 1.0 add_select_fusion.8
  71.0 0.9 add_select_fusion.9
  71.9 1.0 add_select_fusion.8
  73.0 0.9 add_select_fusion.9
  73.9 1.0 add_select_fusion.8
  75.0 0.9 add_select_fusion.9
  76.0 1.0 add_select_fusion.8
  77.0 0.9 add_select_fusion.9
  78.0 1.0 add_select_fusion.8
  79.0 0.9 add_select_fusion.9
  80.0 1.0 add_select_fusion.8
  81.0 0.9 add_select_fusion.9
  82.0 1.0 add_select_fusion.8
  83.1 0.7 add_select_fusion.5
  83.7 0.7 add_select_fusion.4
  84.5 54.6 %all-reduce.3.cloned.1.call-done = (f32[1,16,4096]{2,1,0:T(8,128)}, f32[1,16,2048]{2,1,0:T(8,128)}) async-done(((f32[1,16,4096]{2,1,0:T(8,128)}, f32[1,16,2048]{2,1,0:T(8,128)}), (f32[1,16,4096]{2,1,0:T(8,128)}, f32[1,16,2048]{2,1,0:T(8,128)})) %all-reduce.3.cloned.1.call-update) | async-done | bytes 393232 | tf_op jit(solution)/shard_map/psum | solution.py:26
  139.2 0.9 constant_dynamic-slice_fusion.1
  140.1 0.9 constant_dynamic-slice_fusion
  140.9 1.0 reshape_reshape.7
  141.9 1.3 slice_add_fusion.1
  143.3 1.3 copy.129
  144.6 1.3 copy.130
  145.9 0.1 copy.131
  146.0 3.5 %reshape_reshape.6 = f32[1,2,32,2,32,2]{5,4,3,2,1,0:T(8,128)} reshape(f32[1,2,4096]{2,1,0:T(2,128)S(1)} %constant_dynamic-slice_fusion.1) | data formatting | bytes 65536 | tf_op jit(solution)/shard_map/reshape;reshape | solution.py:32
  149.5 3.4 %fusion.5 = (f32[2,32,32]{2,1,0:T(8,128)S(1)}, f32[2,32,32]{2,1,0:T(8,128)S(1)}) fusion(f32[1,2,32,2,32,2]{5,4,3,2,1,0:T(8,128)} %reshape_reshape.6), kind=kLoop, calls=%fused_computation.10 | loop fusion | flops 4096 | bytes 49152 | tf_op jit(solution)/shard_map/sub | solution.py:34
  153.0 3.0 %copy.146 = f32[1,2,32,2,32,2]{3,2,5,4,1,0:T(8,128)} copy(f32[1,2,32,2,32,2]{4,2,1,5,3,0:T(8,128)S(1)} %pad_maximum_fusion) | data formatting | bytes 65536 | tf_op jit(solution)/shard_map/reshape | solution.py:49
  156.0 3.3 %reshape.321 = f32[1,2,64,64]{2,3,1,0:T(8,128)S(1)} reshape(f32[1,2,32,2,32,2]{3,2,5,4,1,0:T(8,128)} %copy.146) | data formatting | bytes 65536 | tf_op jit(solution)/shard_map/reshape | solution.py:49
  159.5 11.7 %custom-call.8 = f32[1,2,64,64]{3,2,1,0:T(8,128)S(1)} custom-call(f32[1,2,64,64]{3,2,1,0:T(8,128)S(1)} %fusion.18), custom_call_target="Cholesky" | custom-call | tf_op jit(solution)/shard_map/jit(cholesky)/cholesky | solution.py:117
  171.3 0.1 compare_reduce_fusion
  171.5 9.8 %custom-call.9 = f32[2,1,64,64]{2,3,1,0:T(8,128)S(1)} custom-call(f32[2,1,64,64]{3,2,1,0:T(8,128)S(1)} %get-tuple-element.154), custom_call_target="InvertDiagBlocksLowerTriangular" | custom-call | tf_op jit(solution)/shard_map/jit(_solve_triangular)/vmap()/triangular_solve | solution.py:118
  181.3 0.3 convolution_bitcast_fusion
  181.6 0.7 reshape.325
  182.3 4.5 %all-to-all-start = ((f32[4,1,512]{2,1,0:T(1,128)}), f32[4,1,512]{2,1,0:T(1,128)S(1)}, u32[]{:S(2)}, u32[]{:S(2)}) async-start(f32[4,1,512]{2,1,0:T(1,128)} %reshape.325), calls=%async_computation | async-start | bytes 16384 | tf_op jit(solution)/shard_map/all_to_all | solution.py:120
  186.8 14.5 %all_gather.11 = f32[4,2,64,64]{3,2,1,0:T(8,128)S(1)} all-gather(f32[1,2,64,64]{3,2,1,0:T(8,128)S(1)} %get-tuple-element.155), channel_id=1, replica_groups=mesh['chain'=8,'par'=4] {'par'}, dimensions={0}, use_global_device_ids=true | all-gather | bytes 163840 | tf_op jit(solution)/shard_map/all_gather | solution.py:119
  201.4 0.5 broadcast.230
  201.9 0.7 reduce.15
  202.7 2.6 %fusion.4 = f32[4,2,4,32,64]{4,3,2,1,0:T(8,128)} fusion(f32[4,2,4,32,64]{3,4,2,1,0:T(8,128)S(1)} %bitcast.64, f32[4,2,64,64]{3,2,1,0:T(8,128)S(1)} %all_gather.11, f32[4,2,4,64]{3,2,1,0:T(4,128)S(1)} %bitcast.69), kind=kOutput, calls=%fused_computation.7 | convolution fusion | flops 50462720 | bytes 663552 | tf_op jit(solution)/shard_map/bsij,bstkj->bstki/dot_general | solution.py:69
  205.3 1.4 copy.138
  206.7 2.3 %reduce_sum.9 = f32[4,2,4,32,32]{3,4,2,1,0:T(8,128)} reduce(f32[4,2,4,32,32,2]{3,5,4,2,1,0:T(2,128)S(1)} %bitcast.65, f32[]{:T(128)} %constant.116.clone.1), dimensions={5}, to_apply=%region_6.7 | reduce | flops 32768 | bytes 393220 | tf_op jit(solution)/shard_map/reduce_sum | solution.py:76
  209.0 1.1 rev.6
  210.1 0.2 copy.139
  210.3 6.1 %reduce_window_sum.11 = f32[4,2,4,32,32]{4,3,2,1,0:T(8,128)S(1)} reduce-window(f32[4,2,4,32,32]{4,3,2,1,0:T(8,128)S(1)} %copy.139, f32[]{:T(128)} %constant.116.clone.1), window={size=1x1x1x1x32 pad=0_0x0_0x0_0x0_0x31_0}, to_apply=%region_7.8 | reduce-window | flops 1015808 | bytes 262148 | tf_op jit(solution)/shard_map/jit(cumsum)/reduce_window_sum | solution.py:78
  216.4 1.0 rev.7
  217.4 1.1 broadcast_multiply_fusion
  218.5 0.9 reshape.319
  (35 shorter events, 0.7 us)
Async XLA Ops:
  6.5 1.6 copy-start
  6.5 30.7 %all-gather.5.cloned.1.call-start = ((), (), s32[]{:S(2)}) async-start(), calls=%async_computation.2 | async-start | bytes 1179648 | tf_op jit(solution)/shard_map/all_gather | solution.py:11
  11.0 55.9 %all-gather.3.cloned.1.call-start = ((), (), s32[]{:S(2)}) async-start(), calls=%async_computation.1 | async-start | bytes 2359296 | tf_op jit(solution)/shard_map/all_gather | solution.py:11
  12.6 126.5 %all-reduce.3.cloned.1.call-start = ((), (), s32[]{:S(2)}) async-start(), calls=%async_computation.3 | async-start | bytes 786432 | tf_op jit(solution)/shard_map/psum | solution.py:26
  16.8 1.5 copy-start.5
  66.9 16.1 %copy-start.3 = (f32[1,16,2048]{2,1,0:T(8,128)S(1)}, f32[1,16,2048]{2,1,0:T(8,128)}, u32[]{:S(2)}) copy-start(f32[1,16,2048]{2,1,0:T(8,128)} %reshape.316) | copy-start | bytes 393220
  66.9 16.8 %copy-start.2 = (f32[1,16,4096]{2,1,0:T(8,128)S(1)}, f32[1,16,4096]{2,1,0:T(8,128)}, u32[]{:S(2)}) copy-start(f32[1,16,4096]{2,1,0:T(8,128)} %reshape.314) | copy-start | bytes 786436
  153.0 6.3 %copy-start.4 = (f32[64,64]{0,1:T(8,128)S(1)}, f32[64,64]{0,1:T(8,128)}, u32[]{:S(2)}) copy-start(f32[64,64]{0,1:T(8,128)} %copy.125) | copy-start | bytes 49156
  156.0 46.7 %copy-start.1 = (f32[4,2,4,32,32,2]{3,5,4,2,1,0:T(2,128)S(1)}, f32[4,2,4,32,32,2]{3,5,4,2,1,0:T(2,128)}, u32[]{:S(2)}) copy-start(f32[4,2,4,32,32,2]{3,5,4,2,1,0:T(2,128)} %copy.136) | copy-start | bytes 786436
  182.3 19.1 %all-to-all-start = ((f32[4,1,512]{2,1,0:T(1,128)}), f32[4,1,512]{2,1,0:T(1,128)S(1)}, u32[]{:S(2)}, u32[]{:S(2)}) async-start(f32[4,1,512]{2,1,0:T(1,128)} %reshape.325), calls=%async_computation | async-start | bytes 16384 | tf_op jit(solution)/shard_map/all_to_all | solution.py:120
Sparse Core Ops, SparseCore 0:
  11.1 26.0 all-gather.4
  39.1 27.7 all-gather.2
  84.6 54.4 all-reduce.2
where the time goes:
time: 227 us; the launch traced here: 226 us
  waiting for transfers between devices  103 us (45%)
  other arithmetic  55 us (24%)
  local copies, waits for them, and re-layouts  29.7 us (13%)
  blocking collectives  14.5 us (6%)
  between operations  13.3 us (6%)
  matrix products  5.48 us (2%)
  starting transfers between devices  4.62 us (2%)
    psum x1, waiting for transfers between devices, from_root(): return lax.psum(block, axis)  54.6 us
    all_gather x2, waiting for transfers between devices, prefix(): everything = jax.tree.map(lambda part: lax.all_gather(part, axis), x)  48.4 us
    select_n x16, other arithmetic, turn(): return jax.tree.map(lambda a, b: jnp.where(reached, a, b), new, before)  15.9 us
    all_gather x1, blocking collectives, local(): cholesky_triangle = lax.all_gather(lower_own, 'par', axis=0, tiled=True)  14.5 us
    another operation x4, other arithmetic, local(): lower_own = jnp.linalg.cholesky(assemble(same_part, cross_part, own_noise))  11.9 us
    another operation x3, other arithmetic, local(): rotated_own = jax.scipy.linalg.solve_triangular(lower_own, rhs, lower=True)  9.93 us
    reshape x2, local copies, waits for them, and re-layouts, assemble(): gram = whole.reshape(same_part.shape[:-2] + (order, order))  6.26 us
    another operation x1, other arithmetic, estimate_transmitted(): jnp.cumsum(squared_errors[..., ::-1], axis=-1)[..., ::-1] / terminal_number  6.14 us
  transfers between devices with their start and end apart: 4, of which 3 were waited for; matrix products, arithmetic and copies ran while one was open for 3% of the time, Pallas kernels for 0%

commit v1 on v0

--- a/solution.py
+++ b/solution.py
@@ -2,6 +2,7 @@
 import jax.numpy as jnp
 from jax import lax
 from jax.sharding import PartitionSpec as P
+from jax.lax import all_gather
 
 constellation_norm = 1.0 / 42.0**0.5
 
@@ -23,7 +24,7 @@
 
 def from_root(block, axis, owner):
     block = jnp.where(lax.axis_index(axis) == owner, block, jnp.zeros_like(block))
-    return lax.psum(block, axis)
+    return all_gather(block, axis_name=axis).sum(axis=0)
 
 
 def fold_stats(raw_gram, raw_cross):

time: 227 us -> 220 us (0.969)
  waiting for transfers between devices: 103 us -> 96.5 us
  local copies, waits for them, and re-layouts: 29.7 us -> 25.7 us
  other arithmetic: 55 us -> 58 us
    psum x1 -> x0, waiting for transfers between devices: 54.6 us -> none  [from_root(): return lax.psum(block, axis)]
    all_gather x0 -> x2, waiting for transfers between devices: none -> 43.1 us  [from_root(): return all_gather(block, axis_name=axis).sum(axis=0)]
    all_gather x2, waiting for transfers between devices: 48.4 us -> 53.3 us  [prefix(): everything = jax.tree.map(lambda part: lax.all_gather(part, axis), x)]
    reduce_sum x0 -> x2, other arithmetic: none -> 3.01 us  [from_root(): return all_gather(block, axis_name=axis).sum(axis=0)]
  transfers between devices with their start and end apart: 4 -> 5, of which waited for: 3 -> 4; matrix products, arithmetic and copies ran while one was open for 3% -> 6% of each run, Pallas kernels for 0% -> 0%
where the time goes in v1:
time: 220 us; the launch traced here: 219 us
  waiting for transfers between devices  96.5 us (44%)
  other arithmetic  58 us (26%)
  local copies, waits for them, and re-layouts  25.7 us (12%)
  blocking collectives  14.6 us (7%)
  between operations  13.4 us (6%)
  matrix products  5.48 us (2%)
  starting transfers between devices  4.73 us (2%)
    all_gather x2, waiting for transfers between devices, prefix(): everything = jax.tree.map(lambda part: lax.all_gather(part, axis), x)  53.3 us
    all_gather x2, waiting for transfers between devices, from_root(): return all_gather(block, axis_name=axis).sum(axis=0)  43.1 us
    select_n x16, other arithmetic, turn(): return jax.tree.map(lambda a, b: jnp.where(reached, a, b), new, before)  15.9 us
    all_gather x1, blocking collectives, local(): cholesky_triangle = lax.all_gather(lower_own, 'par', axis=0, tiled=True)  14.6 us
    another operation x4, other arithmetic, local(): lower_own = jnp.linalg.cholesky(assemble(same_part, cross_part, own_noise))  11.9 us
    another operation x3, other arithmetic, local(): rotated_own = jax.scipy.linalg.solve_triangular(lower_own, rhs, lower=True)  9.93 us
    reshape x2, local copies, waits for them, and re-layouts, assemble(): gram = whole.reshape(same_part.shape[:-2] + (order, order))  6.26 us
    another operation x1, other arithmetic, estimate_transmitted(): jnp.cumsum(squared_errors[..., ::-1], axis=-1)[..., ::-1] / terminal_number  6.14 us
  transfers between devices with their start and end apart: 5, of which 4 were waited for; matrix products, arithmetic and copies ran while one was open for 6% of the time, Pallas kernels for 0%

profile of v1, /device:TPU:0, one launch (start us, length us, event | category | flops | bytes accessed | tf_op | source)
XLA Modules:
  0.0 218.6 jit_solution(17466983416309041919)
XLA Ops:
  6.5 1.6 copy-done
  8.1 1.9 fusion
  10.0 0.9 all_gather_reshape.7
  11.0 0.7 fusion.2
  11.7 0.9 all_gather_reshape.6
  12.7 0.9 reshape.322
  13.6 23.6 %all-gather.9.cloned.1.call-done = f32[8,1,16,2048]{3,2,1,0:T(8,128)} async-done(((f32[1,1,16,2048]{3,2,1,0:T(8,128)}), f32[8,1,16,2048]{3,2,1,0:T(8,128)}) %all-gather.9.cloned.1.call-update) | async-done | bytes 1048592 | tf_op jit(solution)/shard_map/all_gather | solution.py:12
  37.2 29.7 %all-gather.7.cloned.1.call-done = f32[8,1,16,4096]{3,2,1,0:T(8,128)} async-done(((f32[1,1,16,4096]{3,2,1,0:T(8,128)}), f32[8,1,16,4096]{3,2,1,0:T(8,128)}) %all-gather.7.cloned.1.call-update) | async-done | bytes 2097168 | tf_op jit(solution)/shard_map/all_gather | solution.py:12
  66.9 16.1 %while.16 = (s32[]{:T(128)}, f32[1,16,4096]{2,1,0:T(8,128)S(1)}, f32[1,16,2048]{2,1,0:T(8,128)S(1)}, s32[]{:T(128)}, f32[8,1,16,4096]{3,2,1,0:T(8,128)}, /*index=5*/f32[8,1,16,2048]{3,2,1,0:T(8,128)}, s32[]{:T(128)}, s32[]{:T(128)}) while((s32[]{:T(128)}, f32[1,16,4096]{2,1,0:T(8,128)S(1)}, f32[1,16,2048]{2,1,0:T(8,128)S(1)}, ...), condition=%wide.region_1.2_spmd.clone, body=%wide.region_0.1_spmd.clone.sunk | while | flops 294916 | bytes 1179771 | solution.py:22
  66.9 1.0 add_select_fusion.9
  67.9 1.0 add_select_fusion.8
  68.9 0.9 add_select_fusion.9
  69.9 1.0 add_select_fusion.8
  71.0 0.9 add_select_fusion.9
  71.9 1.0 add_select_fusion.8
  73.0 0.9 add_select_fusion.9
  73.9 1.0 add_select_fusion.8
  75.0 0.9 add_select_fusion.9
  75.9 1.0 add_select_fusion.8
  77.0 0.9 add_select_fusion.9
  78.0 1.0 add_select_fusion.8
  79.0 0.9 add_select_fusion.9
  80.0 1.0 add_select_fusion.8
  81.0 0.9 add_select_fusion.9
  82.0 1.0 add_select_fusion.8
  83.0 0.7 add_select_fusion.5
  83.8 0.2 reshape.320
  84.0 0.7 add_select_fusion.4
  84.9 0.2 reshape.323
  85.0 0.5 fusion.10
  85.6 0.2 maximum_multiply_fusion
  85.8 1.3 copy.136
  87.1 0.2 dynamic-slice_reduce_fusion
  87.3 20.0 %all-gather.13.cloned.1.call-done = f32[8,16,2048]{2,1,0:T(8,128)} async-done(((f32[1,16,2048]{2,1,0:T(8,128)}), f32[8,16,2048]{2,1,0:T(8,128)}) %all-gather.13.cloned.1.call-update) | async-done | bytes 1048592 | tf_op jit(solution)/shard_map/all_gather | solution.py:27
  107.3 1.3 reduce.12
  108.6 1.0 reshape_reshape.7
  109.6 1.3 slice_add_fusion.1
  110.9 1.3 copy.129
  112.3 1.3 copy.130
  113.6 0.1 copy.131
  113.7 23.1 %all-gather.11.cloned.1.call-done = f32[8,16,4096]{2,1,0:T(8,128)} async-done(((f32[1,16,4096]{2,1,0:T(8,128)}), f32[8,16,4096]{2,1,0:T(8,128)}) %all-gather.11.cloned.1.call-update) | async-done | bytes 2097168 | tf_op jit(solution)/shard_map/all_gather | solution.py:27
  136.8 1.7 reduce.11
  138.6 3.5 %reshape_reshape.6 = f32[1,2,32,2,32,2]{5,4,3,2,1,0:T(8,128)} reshape(f32[2,4096]{1,0:T(2,128)S(1)} %constant_dynamic-slice_fusion.1) | data formatting | bytes 65536 | tf_op jit(solution)/shard_map/reshape;reshape | solution.py:33
  142.1 3.4 %fusion.5 = (f32[2,32,32]{2,1,0:T(8,128)S(1)}, f32[2,32,32]{2,1,0:T(8,128)S(1)}) fusion(f32[1,2,32,2,32,2]{5,4,3,2,1,0:T(8,128)} %reshape_reshape.6), kind=kLoop, calls=%fused_computation.10 | loop fusion | flops 4096 | bytes 49152 | tf_op jit(solution)/shard_map/sub | solution.py:35
  145.6 3.0 %copy.146 = f32[1,2,32,2,32,2]{3,2,5,4,1,0:T(8,128)} copy(f32[1,2,32,2,32,2]{4,2,1,5,3,0:T(8,128)S(1)} %pad_maximum_fusion) | data formatting | bytes 65536 | tf_op jit(solution)/shard_map/reshape | solution.py:50
  148.5 3.3 %reshape.331 = f32[1,2,64,64]{2,3,1,0:T(8,128)S(1)} reshape(f32[1,2,32,2,32,2]{3,2,5,4,1,0:T(8,128)} %copy.146) | data formatting | bytes 65536 | tf_op jit(solution)/shard_map/reshape | solution.py:50
  152.1 11.7 %custom-call.8 = f32[1,2,64,64]{3,2,1,0:T(8,128)S(1)} custom-call(f32[1,2,64,64]{3,2,1,0:T(8,128)S(1)} %fusion.18), custom_call_target="Cholesky" | custom-call | tf_op jit(solution)/shard_map/jit(cholesky)/cholesky | solution.py:118
  163.8 0.1 compare_reduce_fusion
  164.1 9.8 %custom-call.9 = f32[2,1,64,64]{2,3,1,0:T(8,128)S(1)} custom-call(f32[2,1,64,64]{3,2,1,0:T(8,128)S(1)} %get-tuple-element.152), custom_call_target="InvertDiagBlocksLowerTriangular" | custom-call | tf_op jit(solution)/shard_map/jit(_solve_triangular)/vmap()/triangular_solve | solution.py:119
  173.9 0.3 convolution_bitcast_fusion
  174.2 0.7 reshape.335
  174.9 4.6 %all-to-all-start = ((f32[4,1,512]{2,1,0:T(1,128)}), f32[4,1,512]{2,1,0:T(1,128)S(1)}, u32[]{:S(2)}, u32[]{:S(2)}) async-start(f32[4,1,512]{2,1,0:T(1,128)} %reshape.335), calls=%async_computation | async-start | bytes 16384 | tf_op jit(solution)/shard_map/all_to_all | solution.py:121
  179.5 14.6 %all_gather.27 = f32[4,2,64,64]{3,2,1,0:T(8,128)S(1)} all-gather(f32[1,2,64,64]{3,2,1,0:T(8,128)S(1)} %get-tuple-element.153), channel_id=1, replica_groups=mesh['chain'=8,'par'=4] {'par'}, dimensions={0}, use_global_device_ids=true | all-gather | bytes 163840 | tf_op jit(solution)/shard_map/all_gather | solution.py:120
  194.0 0.5 broadcast.230
  194.6 0.7 reduce.21
  195.3 2.6 %fusion.4 = f32[4,2,4,32,64]{4,3,2,1,0:T(8,128)} fusion(f32[4,2,4,32,64]{3,4,2,1,0:T(8,128)S(1)} %bitcast.64, f32[4,2,64,64]{3,2,1,0:T(8,128)S(1)} %all_gather.27, f32[4,2,4,64]{3,2,1,0:T(4,128)S(1)} %bitcast.69), kind=kOutput, calls=%fused_computation.7 | convolution fusion | flops 50462720 | bytes 663552 | tf_op jit(solution)/shard_map/bsij,bstkj->bstki/dot_general | solution.py:70
  197.9 1.4 copy.138
  199.3 2.3 %reduce_sum.29 = f32[4,2,4,32,32]{3,4,2,1,0:T(8,128)} reduce(f32[4,2,4,32,32,2]{3,5,4,2,1,0:T(2,128)S(1)} %bitcast.65, f32[]{:T(128)} %constant.116.clone.1), dimensions={5}, to_apply=%region_6.7 | reduce | flops 32768 | bytes 393220 | tf_op jit(solution)/shard_map/reduce_sum | solution.py:77
  201.7 1.1 rev.6
  202.7 0.2 copy.139
  203.0 6.1 %reduce_window_sum.11 = f32[4,2,4,32,32]{4,3,2,1,0:T(8,128)S(1)} reduce-window(f32[4,2,4,32,32]{4,3,2,1,0:T(8,128)S(1)} %copy.139, f32[]{:T(128)} %constant.116.clone.1), window={size=1x1x1x1x32 pad=0_0x0_0x0_0x0_0x31_0}, to_apply=%region_7.8 | reduce-window | flops 1015808 | bytes 262148 | tf_op jit(solution)/shard_map/jit(cumsum)/reduce_window_sum | solution.py:79
  209.1 1.0 rev.7
  210.1 1.1 broadcast_multiply_fusion
  211.2 0.9 reshape.325
  (38 shorter events, 0.9 us)
Async XLA Ops:
  6.5 1.6 copy-start
  6.5 30.7 %all-gather.9.cloned.1.call-start = ((), (), s32[]{:S(2)}) async-start(), calls=%async_computation.2 | async-start | bytes 1179648 | tf_op jit(solution)/shard_map/all_gather | solution.py:12
  11.0 55.9 %all-gather.7.cloned.1.call-start = ((), (), s32[]{:S(2)}) async-start(), calls=%async_computation.1 | async-start | bytes 2359296 | tf_op jit(solution)/shard_map/all_gather | solution.py:12
  12.6 94.6 %all-gather.13.cloned.1.call-start = ((), (), s32[]{:S(2)}) async-start(), calls=%async_computation.4 | async-start | bytes 1179648 | tf_op jit(solution)/shard_map/all_gather | solution.py:27
  66.9 16.1 %copy-start.2 = (f32[1,16,2048]{2,1,0:T(8,128)S(1)}, f32[1,16,2048]{2,1,0:T(8,128)}, u32[]{:S(2)}) copy-start(f32[1,16,2048]{2,1,0:T(8,128)} %reshape.322) | copy-start | bytes 393220
  83.0 1.8 copy-start.3
  83.7 53.1 %all-gather.11.cloned.1.call-start = ((), (), s32[]{:S(2)}) async-start(), calls=%async_computation.3 | async-start | bytes 2359296 | tf_op jit(solution)/shard_map/all_gather | solution.py:27
  85.6 1.5 copy-start.4
  148.5 46.8 %copy-start.1 = (f32[4,2,4,32,32,2]{3,5,4,2,1,0:T(2,128)S(1)}, f32[4,2,4,32,32,2]{3,5,4,2,1,0:T(2,128)}, u32[]{:S(2)}) copy-start(f32[4,2,4,32,32,2]{3,5,4,2,1,0:T(2,128)} %copy.136) | copy-start | bytes 786436
  174.9 19.2 %all-to-all-start = ((f32[4,1,512]{2,1,0:T(1,128)}), f32[4,1,512]{2,1,0:T(1,128)S(1)}, u32[]{:S(2)}, u32[]{:S(2)}) async-start(f32[4,1,512]{2,1,0:T(1,128)} %reshape.335), calls=%async_computation | async-start | bytes 16384 | tf_op jit(solution)/shard_map/all_to_all | solution.py:121
Sparse Core Ops, SparseCore 0:
  11.1 26.0 all-gather.8
  39.1 27.7 all-gather.6
  83.9 23.3 all-gather.12
  109.0 27.7 all-gather.10
